TPU v7x, 32 devices: a whole 2x2x4 slice. The times are simulated.
32 devices in a mesh: fsdp: 4 (over z), tp: 8 (over y, x, core).
Axes of the slice: x: 2, y: 2, z: 4, core: 2. Of those that a mesh axis runs over, the one named last changes fastest.
Arguments:
- tokens: bfloat16 [3008, 4096], P('fsdp', 'tp'), may hold values from -6 to 6
- norm_gain: float32 [4096], replicated, may hold values from 0.5 to 1.5
- base_gate: bfloat16 [4096, 12288], P(None, 'tp'), may hold values from -0.09375 to 0.09375
- base_up: bfloat16 [4096, 12288], P(None, 'tp'), may hold values from -0.09375 to 0.09375
- base_down: bfloat16 [12288, 4096], P('tp'), may hold values from -0.0546875 to 0.0546875
- code_gate: bfloat16 [4096, 12288], P(('fsdp', 'tp')), may hold values from -4 to 4
- code_up: bfloat16 [4096, 12288], P(('fsdp', 'tp')), may hold values from -4 to 4
- scale_gate: float32 [4096, 96], P(('fsdp', 'tp')), may hold values from 0.005 to 0.05
- scale_up: float32 [4096, 96], P(('fsdp', 'tp')), may hold values from 0.005 to 0.05
- code_down: bfloat16 [12288, 4096], P(None, ('fsdp', 'tp')), may hold values from -4 to 4
- scale_down: float32 [96, 4096], P(None, ('fsdp', 'tp')), may hold values from 0.005 to 0.05
- cu_seqlens: int32 [4, 9], P('fsdp'), may hold values from 0 to 752, as said below
Outputs:
- mixed: bfloat16 [3008, 4096], P('fsdp', 'tp')
- seq_means: float32 [32, 4096], P('fsdp', 'tp')
Inputs may be any that keep to these rules, and one draw needn't show every extreme that they name: `cu_seqlens`: each row starts at 0 and rises strictly; its last entry is the group's live tokens, which fill the first slots of its 752. Over all groups the live tokens add up to exactly 1536, and some group has exactly 752.
All inputs are finite; a program needn't handle non-finite values.
Results may differ from a plain program's by a relative error of at most 0.023.
Values may be sent and summed in bfloat16 or wider, within the bound.
A program may use at most 256 MiB of HBM per device.

v0:
```python
import jax
import jax.numpy as jnp
from jax import lax
from jax.sharding import PartitionSpec as P

SEQS = 8
EPSILON = 1e-06
F32, BF16 = (jnp.float32, jnp.bfloat16)


def dequant_rows(base_part, code_part, scales):
    rows, cols = code_part.shape
    blocks = scales.shape[1]
    delta = code_part.astype(F32).reshape(rows, blocks, cols // blocks) * scales[:, :, None]
    return (base_part.astype(F32) + delta.reshape(rows, cols)).astype(BF16)


def dequant_cols(base_part, code_part, scales):
    rows, cols = code_part.shape
    blocks = scales.shape[0]
    delta = code_part.astype(F32).reshape(blocks, rows // blocks, cols) * scales[:, None, :]
    return (base_part.astype(F32) + delta.reshape(rows, cols)).astype(BF16)


def swap_up(part, axis_name="tp"):
    return lax.all_to_all(part, axis_name, split_axis=1, concat_axis=0, tiled=True)


def swap_down(part):
    return lax.all_to_all(part, "tp", split_axis=0, concat_axis=1, tiled=True)


def shards(
    tokens,
    norm_gain,
    base_gate,
    base_up,
    base_down,
    code_gate,
    code_up,
    scale_gate,
    scale_up,
    code_down,
    scale_down,
    cu_seqlens,
):
    groups = lax.axis_size("fsdp")
    slices = lax.axis_size("tp")
    me_f = lax.axis_index("fsdp")
    me_t = lax.axis_index("tp")
    cap, feat = tokens.shape
    width = base_gate.shape[0]
    depth = width // groups
    units = base_gate.shape[1]
    live_all = groups * (cap // 2 + SEQS)
    grain = 16 * slices
    capp = -(-cap // grain) * grain
    part = capp // slices
    padded = jnp.pad(tokens, ((0, capp - cap), (0, 0)))
    rows_full = lax.all_to_all(padded, "tp", split_axis=0, concat_axis=1, tiled=True)
    wide = rows_full.astype(F32)
    inverse = lax.rsqrt(jnp.mean(wide * wide, axis=1, keepdims=True) + EPSILON)
    normed = (wide * inverse * norm_gain[None, :]).astype(BF16)
    block = swap_up(normed, "fsdp")
    every = lax.all_gather(block, "tp", axis=0, tiled=True)
    bounds_all = lax.all_gather(cu_seqlens, "fsdp", axis=0, tiled=True)
    counts = bounds_all[:, SEQS]
    ends = jnp.cumsum(counts)
    starts = ends - counts
    place = jnp.arange(live_all, dtype=jnp.int32)
    group_of = jnp.sum((place[:, None] >= ends[None, :]).astype(jnp.int32), axis=1)
    group_of = jnp.minimum(group_of, groups - 1)
    slot = place - jnp.take(starts, group_of)
    source = slot // part * (groups * part) + group_of * part + slot % part
    pick = (source[:, None] == jnp.arange(slices * groups * part, dtype=jnp.int32)[None, :]).astype(
        BF16
    )
    packed = jnp.dot(pick, every, preferred_element_type=F32).astype(BF16)
    gate_rows = lax.dynamic_slice_in_dim(base_gate, me_f * depth, depth, 0)
    up_rows = lax.dynamic_slice_in_dim(base_up, me_f * depth, depth, 0)
    w_gate = dequant_rows(gate_rows, swap_up(code_gate), swap_up(scale_gate))
    w_up = dequant_rows(up_rows, swap_up(code_up), swap_up(scale_up))
    gate_part = jnp.dot(packed, w_gate, preferred_element_type=F32).astype(BF16)
    up_part = jnp.dot(packed, w_up, preferred_element_type=F32).astype(BF16)
    up_part, code_down = lax.optimization_barrier((up_part, code_down))
    gate_sum = lax.psum_scatter(gate_part, "fsdp", scatter_dimension=0, tiled=True)
    up_sum = lax.psum_scatter(up_part, "fsdp", scatter_dimension=0, tiled=True)
    down_codes, down_scales = (swap_down(code_down), swap_down(scale_down))
    gate_sum, up_sum, down_codes, down_scales = lax.optimization_barrier(
        (gate_sum, up_sum, down_codes, down_scales)
    )
    hidden = (jax.nn.silu(gate_sum.astype(F32)) * up_sum.astype(F32)).astype(BF16)
    hidden_all = lax.all_gather(hidden, "fsdp", axis=0, tiled=True)
    down_cols = lax.dynamic_slice_in_dim(base_down, me_f * depth, depth, 1)
    w_down = dequant_cols(down_cols, down_codes, down_scales)
    out_part = jnp.dot(hidden_all, w_down, preferred_element_type=F32).astype(BF16)
    out_cols = lax.psum_scatter(out_part, "tp", scatter_dimension=1, tiled=True)
    narrow = out_cols.shape[1]
    grp = jnp.arange(groups, dtype=jnp.int32)
    slots = jnp.arange(cap, dtype=jnp.int32)
    wanted = jnp.where(slots[None, :] < counts[:, None], starts[:, None] + slots[None, :], -1)
    spread = (wanted.reshape(-1)[:, None] == place[None, :]).astype(BF16)
    placed_rows = jnp.dot(spread, out_cols, preferred_element_type=F32).astype(BF16)
    mine = lax.all_to_all(
        placed_rows.reshape(groups, cap, narrow), "fsdp", split_axis=0, concat_axis=0, tiled=True
    )
    ratio = slices // groups
    span = slices // ratio
    half = me_t // span
    pick_half = (jnp.arange(ratio) == half)[None, :, None, None]
    outgoing = jnp.where(pick_half, mine[:, None], jnp.zeros((), BF16)).reshape(slices, cap, narrow)
    incoming = lax.all_to_all(outgoing, "tp", split_axis=0, concat_axis=0, tiled=True)
    take_from = lax.dynamic_slice_in_dim(incoming, me_t % ratio * span, span, 0)
    summed_out = take_from.transpose(1, 0, 2).reshape(cap, feat).astype(F32)
    bounds = cu_seqlens[0]
    live_count = bounds[SEQS]
    mixed = (tokens.astype(F32) + summed_out).astype(BF16)
    mixed = jnp.where((slots < live_count)[:, None], mixed, jnp.zeros((), BF16))
    member = (slots[None, :] >= bounds[:-1, None]) & (slots[None, :] < bounds[1:, None])
    seq_sums = jnp.dot(member.astype(BF16), mixed, preferred_element_type=F32)
    lengths = (bounds[1:] - bounds[:-1]).astype(F32)
    return (mixed, seq_sums / lengths[:, None])


def solution(mesh):
    placed = (
        P("fsdp", "tp"),
        P(),
        P(None, "tp"),
        P(None, "tp"),
        P("tp", None),
        P(("fsdp", "tp"), None),
        P(("fsdp", "tp"), None),
        P(("fsdp", "tp"), None),
        P(("fsdp", "tp"), None),
        P(None, ("fsdp", "tp")),
        P(None, ("fsdp", "tp")),
        P("fsdp", None),
    )
    return jax.shard_map(
        shards,
        mesh=mesh,
        in_specs=placed,
        out_specs=(P("fsdp", "tp"), P("fsdp", "tp")),
        check_vma=False,
    )
```

profile of v0, /device:TPU:0, one launch (start us, length us, event | category | flops | bytes accessed | tf_op | source)
XLA Modules:
  0.0 536.5 jit_solution(2134350978414402686)
XLA Ops:
  7.2 2.1 pad.4
  9.3 5.2 all-to-all-start
  15.2 11.8 %all-to-all-done = bf16[8,96,512]{2,1,0:T(8,128)(2,1)S(1)} async-done(((bf16[8,96,512]{2,1,0:T(8,128)(2,1)}), bf16[8,96,512]{2,1,0:T(8,128)(2,1)S(1)}, u32[]{:S(2)}, u32[]{:S(2)}) %all-to-all-start) | async-done | bytes 786464 | tf_op jit(solution)/shard_map/all_to_all | solution.py:60
  28.1 1.9 reshape.196
  30.4 2.0 multiply_convert_fusion
  32.6 22.1 %all_to_all.135 = bf16[96,4,1024]{2,0,1:T(8,128)(2,1)} all-to-all(bf16[96,4,1024]{2,0,1:T(8,128)(2,1)S(1)} %copy.58), channel_id=1, replica_groups=mesh['fsdp'=4,'tp'=8] {'fsdp'}, dimensions={1} | all-to-all | bytes 1572864 | tf_op jit(solution)/shard_map/all_to_all | solution.py:26
  55.4 4.8 all-to-all-start.3
  60.2 2.9 copy.60
  63.0 2.2 all-to-all-done.3
  65.2 4.6 all-to-all-start.2
  69.9 9.2 %all-gather = s32[4,1,9]{2,1,0:T(1,128)S(1)} all-gather(s32[1,1,9]{2,1,0:T(1,128)S(1)} %bitcast.123), channel_id=1, replica_groups=mesh['fsdp'=4,'tp'=8] {'fsdp'}, dimensions={0}, use_global_device_ids=true | all-gather | bytes 180 | tf_op jit(solution)/shard_map/all_gather | solution.py:66
  79.2 2.1 constant_dynamic-slice_fusion.1
  81.3 2.9 copy.73
  85.1 2.5 fusion.29
  87.7 34.9 %all-to-all-done.2 = bf16[128,8,1536]{0,2,1:T(8,128)(2,1)} async-done(((bf16[128,8,1536]{0,2,1:T(8,128)(2,1)}), bf16[128,8,1536]{0,2,1:T(8,128)(2,1)}, u32[]{:S(2)}, u32[]{:S(2)}) %all-to-all-start.2) | async-done | bytes 3145760 | tf_op jit(solution)/shard_map/all_to_all | solution.py:26
  122.6 3.9 fusion.7
  126.6 12.5 %fusion.10 = bf16[1536,1024]{1,0:T(8,128)(2,1)S(1)} fusion(bf16[3072,1024]{1,0:T(8,128)(2,1)} %all-gather.4.cloned.1.call-done, s32[1536]{0:T(1024)S(1)} %fusion.27), kind=kOutput, calls=%fused_computation.20 | convolution fusion | flops 9669967872 | bytes 9443328 | tf_op jit(solution)/shard_map/dot_general | solution.py:78
  139.1 1.6 copy-done.8
  140.8 6.9 %convolution_convert_fusion.1 = bf16[1536,1536]{1,0:T(8,128)(2,1)} fusion(bf16[1536,1024]{1,0:T(8,128)(2,1)S(1)} %fusion.10, bf16[1024,1536]{0,1:T(8,128)(2,1)S(1)} %fusion.7), kind=kOutput, calls=%fused_computation.7 | convolution fusion | flops 4834197504 | bytes 11010048 | tf_op jit(solution)/shard_map/dot_general | solution.py:83
  149.1 3.4 all-to-all-start.5
  152.5 2.8 copy.64
  155.3 2.1 all-to-all-done.5
  157.4 4.5 all-to-all-start.4
  162.2 2.1 constant_dynamic-slice_fusion
  164.3 2.9 copy.74
  167.2 32.5 %all-to-all-done.4 = bf16[128,8,1536]{0,2,1:T(8,128)(2,1)} async-done(((bf16[128,8,1536]{0,2,1:T(8,128)(2,1)}), bf16[128,8,1536]{0,2,1:T(8,128)(2,1)}, u32[]{:S(2)}, u32[]{:S(2)}) %all-to-all-start.4) | async-done | bytes 3145760 | tf_op jit(solution)/shard_map/all_to_all | solution.py:26
  199.8 4.0 fusion.5
  203.8 6.9 %convolution_convert_fusion = bf16[1536,1536]{1,0:T(8,128)(2,1)} fusion(bf16[1536,1024]{1,0:T(8,128)(2,1)S(1)} %copy-done.9, bf16[1024,1536]{0,1:T(8,128)(2,1)S(1)} %fusion.5), kind=kOutput, calls=%fused_computation.6 | convolution fusion | flops 4834197504 | bytes 11010048 | tf_op jit(solution)/shard_map/dot_general | solution.py:84
  211.5 7.4 %all_to_all.136 = f32[8,12,128]{2,1,0:T(8,128)S(1)} all-to-all(f32[8,12,128]{2,1,0:T(8,128)S(1)} %all_to_all.119), channel_id=1, replica_groups=mesh['fsdp'=4,'tp'=8] {'tp'}, dimensions={0} | all-to-all | bytes 98304 | tf_op jit(solution)/shard_map/all_to_all | solution.py:30
  218.9 3.7 all-to-all-start.6
  222.7 37.7 %all-to-all-done.6 = bf16[8,1536,128]{2,1,0:T(8,128)(2,1)S(1)} async-done(((bf16[8,1536,128]{2,1,0:T(8,128)(2,1)}), bf16[8,1536,128]{2,1,0:T(8,128)(2,1)S(1)}, u32[]{:S(2)}, u32[]{:S(2)}) %all-to-all-start.6) | async-done | bytes 3145760 | tf_op jit(solution)/shard_map/all_to_all | solution.py:30
  260.3 2.1 copy_bitcast_fusion
  262.5 58.8 %reduce-scatter.8.cloned.1.call-done = bf16[384,1536]{1,0:T(8,128)(2,1)} async-done(((bf16[1536,1536]{1,0:T(8,128)(2,1)}), bf16[384,1536]{1,0:T(8,128)(2,1)}) %reduce-scatter.8.cloned.1.call-update) | async-done | bytes 1179664 | tf_op jit(solution)/shard_map/reduce_scatter | solution.py:87
  321.3 3.4 fusion.16
  324.8 5.1 fusion.9
  329.9 84.9 %all-gather.6.cloned.1.call-done = bf16[1536,1536]{1,0:T(8,128)(2,1)} async-done(((bf16[384,1536]{1,0:T(8,128)(2,1)}), bf16[1536,1536]{1,0:T(8,128)(2,1)}) %all-gather.6.cloned.1.call-update) | async-done | bytes 4718608 | tf_op jit(solution)/shard_map/all_gather | solution.py:93
  414.8 8.1 %convolution_convert_fusion.2 = bf16[1536,1024]{1,0:T(8,128)(2,1)S(1)} fusion(bf16[1536,1536]{1,0:T(8,128)(2,1)} %all-gather.6.cloned.1.call-done, bf16[1536,1024]{1,0:T(8,128)(2,1)} %fusion.9), kind=kOutput, calls=%fused_computation.19 | convolution fusion | flops 4833411072 | bytes 11010048 | tf_op jit(solution)/shard_map/dot_general | solution.py:96
  422.9 3.0 copy.71
  426.0 44.5 %reduce-scatter.10.cloned.1.call-done = bf16[128,1536]{1,0:T(8,128)(2,1)} async-done(((bf16[1024,1536]{1,0:T(8,128)(2,1)}), bf16[128,1536]{1,0:T(8,128)(2,1)}) %reduce-scatter.10.cloned.1.call-update) | async-done | bytes 393232
  470.5 5.5 %fusion.11 = bf16[3008,128]{1,0:T(8,128)(2,1)} fusion(s32[3008]{0:T(1024)S(1)} %select_n.86, bf16[128,1536]{1,0:T(8,128)(2,1)} %reduce-scatter.10.cloned.1.call-done), kind=kOutput, calls=%fused_computation.21 | convolution fusion | flops 1187799040 | bytes 1175296 | tf_op jit(solution)/shard_map/dot_general | solution.py:103
  476.0 4.7 all-to-all-start.8
  480.9 19.5 %all-to-all-done.8 = bf16[4,752,128]{2,1,0:T(8,128)(2,1)S(1)} async-done(((bf16[4,752,128]{2,1,0:T(8,128)(2,1)}), bf16[4,752,128]{2,1,0:T(8,128)(2,1)S(1)}, u32[]{:S(2)}, u32[]{:S(2)}) %all-to-all-start.8) | async-done | bytes 770080 | tf_op jit(solution)/shard_map/all_to_all | solution.py:104
  500.4 1.3 bitcast_select_fusion
  501.7 3.6 all-to-all-start.9
  505.3 1.2 copy.56
  507.8 18.0 %all-to-all-done.9 = bf16[8,752,128]{2,1,0:T(8,128)(2,1)S(1)} async-done(((bf16[8,752,128]{2,1,0:T(8,128)(2,1)}), bf16[8,752,128]{2,1,0:T(8,128)(2,1)S(1)}, u32[]{:S(2)}, u32[]{:S(2)}) %all-to-all-start.9) | async-done | bytes 1540128 | tf_op jit(solution)/shard_map/all_to_all | solution.py:112
  526.4 1.4 fusion.19
  527.9 1.2 copy.70
  (69 shorter events, 10.1 us)
Async XLA Ops:
  9.3 17.8 %all-to-all-start = ((bf16[8,96,512]{2,1,0:T(8,128)(2,1)}), bf16[8,96,512]{2,1,0:T(8,128)(2,1)S(1)}, u32[]{:S(2)}, u32[]{:S(2)}) async-start(bf16[8,96,512]{2,1,0:T(8,128)(2,1)} %bitcast.7), calls=%async_computation | async-start | bytes 1572864 | tf_op jit(solution)/shard_map/all_to_all | solution.py:60
  14.5 112.1 %all-gather.4.cloned.1.call-start = ((), (), s32[]{:S(2)}) async-start(), calls=%async_computation.13 | async-start | bytes 7077888 | tf_op jit(solution)/shard_map/all_gather | solution.py:65
  30.3 24.4 %copy-start.4 = (f32[128,96]{0,1:T(8,128)S(1)}, f32[128,96]{0,1:T(8,128)}, u32[]{:S(2)}) copy-start(f32[128,96]{0,1:T(8,128)} %param.19) | copy-start | bytes 147460
  30.4 29.8 %copy-start.1 = (bf16[128,12288]{1,0:T(8,128)(2,1)S(1)}, bf16[128,12288]{1,0:T(8,128)(2,1)}, u32[]{:S(2)}) copy-start(bf16[128,12288]{1,0:T(8,128)(2,1)} %param.17) | copy-start | bytes 9437188
  55.4 9.8 %all-to-all-start.3 = ((f32[128,8,12]{0,2,1:T(8,128)}), f32[128,8,12]{0,2,1:T(8,128)S(1)}, u32[]{:S(2)}, u32[]{:S(2)}) async-start(f32[128,8,12]{0,2,1:T(8,128)} %all_to_all.107), calls=%async_computation.3 | async-start | bytes 131072 | tf_op jit(solution)/shard_map/all_to_all | solution.py:26
  65.2 4.7 copy-start.7
  65.2 57.4 %all-to-all-start.2 = ((bf16[128,8,1536]{0,2,1:T(8,128)(2,1)}), bf16[128,8,1536]{0,2,1:T(8,128)(2,1)}, u32[]{:S(2)}, u32[]{:S(2)}) async-start(bf16[128,8,1536]{0,2,1:T(8,128)(2,1)} %bitcast.11), calls=%async_computation.2 | async-start | bytes 6291456 | tf_op jit(solution)/shard_map/all_to_all | solution.py:26
  69.8 192.6 %reduce-scatter.6.cloned.1.call-start = ((), (), s32[]{:S(2)}) async-start(), calls=%async_computation.14 | async-start | bytes 5898240 | tf_op jit(solution)/shard_map/reduce_scatter | solution.py:86
  139.1 1.6 copy-start.8
  147.7 0.8 copy-start.5
  147.7 4.8 copy-start.2
  149.1 8.3 %all-to-all-start.5 = ((f32[128,8,12]{0,2,1:T(8,128)}), f32[128,8,12]{0,2,1:T(8,128)S(1)}, u32[]{:S(2)}, u32[]{:S(2)}) async-start(f32[128,8,12]{0,2,1:T(8,128)} %all_to_all.112), calls=%async_computation.6 | async-start | bytes 131072 | tf_op jit(solution)/shard_map/all_to_all | solution.py:26
  157.4 42.4 %all-to-all-start.4 = ((bf16[128,8,1536]{0,2,1:T(8,128)(2,1)}), bf16[128,8,1536]{0,2,1:T(8,128)(2,1)}, u32[]{:S(2)}, u32[]{:S(2)}) async-start(bf16[128,8,1536]{0,2,1:T(8,128)(2,1)} %bitcast.15), calls=%async_computation.5 | async-start | bytes 6291456 | tf_op jit(solution)/shard_map/all_to_all | solution.py:26
  161.9 159.4 %reduce-scatter.8.cloned.1.call-start = ((), (), s32[]{:S(2)}) async-start(), calls=%async_computation.15 | async-start | bytes 5898240 | tf_op jit(solution)/shard_map/reduce_scatter | solution.py:87
  199.8 4.0 copy-start.9
  210.7 0.8 copy-start.6
  218.9 41.4 %all-to-all-start.6 = ((bf16[8,1536,128]{2,1,0:T(8,128)(2,1)}), bf16[8,1536,128]{2,1,0:T(8,128)(2,1)S(1)}, u32[]{:S(2)}, u32[]{:S(2)}) async-start(bf16[8,1536,128]{2,1,0:T(8,128)(2,1)} %bitcast.108), calls=%async_computation.8 | async-start | bytes 6291456 | tf_op jit(solution)/shard_map/all_to_all | solution.py:30
  222.5 192.2 %all-gather.6.cloned.1.call-start = ((), (), s32[]{:S(2)}) async-start(), calls=%async_computation.16 | async-start | bytes 5898240 | tf_op jit(solution)/shard_map/all_gather | solution.py:93
  262.4 62.3 %copy-start = (bf16[1536,1024]{1,0:T(8,128)(2,1)S(1)}, bf16[1536,1024]{1,0:T(8,128)(2,1)}, u32[]{:S(2)}) copy-start(bf16[1536,1024]{1,0:T(8,128)(2,1)} %copy_bitcast_fusion) | copy-start | bytes 9437188
  324.7 145.8 %reduce-scatter.10.cloned.1.call-start = ((), (), s32[]{:S(2)}) async-start(), calls=%async_computation.17 | async-start | bytes 3538944
  476.0 29.2 %copy-start.3 = (bf16[752,512]{1,0:T(8,128)(2,1)S(1)}, bf16[752,512]{1,0:T(8,128)(2,1)}, u32[]{:S(2)}) copy-start(bf16[752,512]{1,0:T(8,128)(2,1)} %param.12) | copy-start | bytes 2310148
  476.0 24.3 %all-to-all-start.8 = ((bf16[4,752,128]{2,1,0:T(8,128)(2,1)}), bf16[4,752,128]{2,1,0:T(8,128)(2,1)S(1)}, u32[]{:S(2)}, u32[]{:S(2)}) async-start(bf16[4,752,128]{2,1,0:T(8,128)(2,1)} %bitcast.23), calls=%async_computation.10 | async-start | bytes 1540096 | tf_op jit(solution)/shard_map/all_to_all | solution.py:104
  501.7 24.2 %all-to-all-start.9 = ((bf16[8,752,128]{2,1,0:T(8,128)(2,1)}), bf16[8,752,128]{2,1,0:T(8,128)(2,1)S(1)}, u32[]{:S(2)}, u32[]{:S(2)}) async-start(bf16[8,752,128]{2,1,0:T(8,128)(2,1)} %bitcast_select_fusion), calls=%async_computation.11 | async-start | bytes 3080192 | tf_op jit(solution)/shard_map/all_to_all | solution.py:112
Sparse Core Ops, SparseCore 0:
  54.9 71.6 all-gather.3
  147.8 85.2 reduce-scatter.5
  235.4 85.7 reduce-scatter.7
  324.8 89.8 all-gather.5
  426.0 44.4 reduce-scatter.9
where the time goes:
time: 538 us; the launch traced here: 536 us
  waiting for transfers between devices  347 us (64%)
  matrix products  40.9 us (8%)
  blocking collectives  38.7 us (7%)
  local copies, waits for them, and re-layouts  35.5 us (7%)
  starting transfers between devices  34.8 us (6%)
  other arithmetic  25.4 us (5%)
  between operations  14.1 us (3%)
    all_gather x1, waiting for transfers between devices, shards(): hidden_all = lax.all_gather(hidden, 'fsdp', axis=0, tiled=True)  84.9 us
    all_to_all x4, waiting for transfers between devices, swap_up(): lax.all_to_all(part, axis_name, split_axis=1, concat_axis=0, tiled=True)  71.8 us
    reduce_scatter x1, waiting for transfers between devices, shards(): up_sum = lax.psum_scatter(up_part, 'fsdp', scatter_dimension=0, tiled=True)  58.8 us
    unnamed x6, waiting for transfers between devices  44.5 us
    all_to_all x1, waiting for transfers between devices, swap_down(): return lax.all_to_all(part, 'tp', split_axis=0, concat_axis=1, tiled=True)  37.7 us
    all_to_all x1, blocking collectives, swap_up(): lax.all_to_all(part, axis_name, split_axis=1, concat_axis=0, tiled=True)  22.1 us
    unnamed x33, local copies, waits for them, and re-layouts  20 us
    all_to_all x1, waiting for transfers between devices, shards(): lax.all_to_all(placed_rows.reshape(groups, cap, narrow), 'fsdp', split_ax...  19.5 us
  transfers between devices with their start and end apart: 13, of which 12 were waited for; matrix products, arithmetic and copies ran while one was open for 8% of the time, Pallas kernels for 0%

commit v1 on v0

--- a/solution.py
+++ b/solution.py
@@ -6,6 +6,17 @@
 SEQS = 8
 EPSILON = 1e-06
 F32, BF16 = (jnp.float32, jnp.bfloat16)
+
+
+def around_the_ring(x, axis, dim):
+    size = lax.axis_size(axis)
+    route = [(i, (i + 1) % size) for i in range(size)]
+    parts = [x]
+    for stride in range(1, size):
+        parts = [lax.ppermute(parts[0], axis, route), *parts]
+    whole = jnp.concatenate(parts, axis=dim)
+    places = (lax.axis_index(axis) + 1) * parts[-1].shape[dim]
+    return jnp.roll(whole, places, axis=dim)
 
 
 def dequant_rows(base_part, code_part, scales):
@@ -90,7 +101,7 @@
         (gate_sum, up_sum, down_codes, down_scales)
     )
     hidden = (jax.nn.silu(gate_sum.astype(F32)) * up_sum.astype(F32)).astype(BF16)
-    hidden_all = lax.all_gather(hidden, "fsdp", axis=0, tiled=True)
+    hidden_all = around_the_ring(hidden, "fsdp", 0)
     down_cols = lax.dynamic_slice_in_dim(base_down, me_f * depth, depth, 1)
     w_down = dequant_cols(down_cols, down_codes, down_scales)
     out_part = jnp.dot(hidden_all, w_down, preferred_element_type=F32).astype(BF16)

time: 538 us -> 538 us (level)
  local copies, waits for them, and re-layouts: 35.5 us -> 43.3 us
    all_gather x1 -> x0, waiting for transfers between devices: 84.9 us -> none  [shards(): hidden_all = lax.all_gather(hidden, 'fsdp', axis=0, tiled=True)]
    ppermute x0 -> x3, waiting for transfers between devices: none -> 81.2 us  [around_the_ring(): parts = [lax.ppermute(parts[0], axis, route), *parts]]
    unnamed x33 -> x48, local copies, waits for them, and re-layouts: 20 us -> 27.7 us
    unnamed x6 -> x5, waiting for transfers between devices: 44.5 us -> 44.3 us
  transfers between devices with their start and end apart: 13 -> 15, of which waited for: 12 -> 14; matrix products, arithmetic and copies ran while one was open for 8% -> 8% of each run, Pallas kernels for 0% -> 0%
where the time goes in v1:
time: 538 us; the launch traced here: 536 us
  waiting for transfers between devices  343 us (64%)
  local copies, waits for them, and re-layouts  43.3 us (8%)
  blocking collectives  38.7 us (7%)
  matrix products  38.1 us (7%)
  starting transfers between devices  36.3 us (7%)
  other arithmetic  22.8 us (4%)
  between operations  14.2 us (3%)
    ppermute x3, waiting for transfers between devices, around_the_ring(): parts = [lax.ppermute(parts[0], axis, route), *parts]  81.2 us
    all_to_all x4, waiting for transfers between devices, swap_up(): lax.all_to_all(part, axis_name, split_axis=1, concat_axis=0, tiled=True)  71.6 us
    reduce_scatter x1, waiting for transfers between devices, shards(): up_sum = lax.psum_scatter(up_part, 'fsdp', scatter_dimension=0, tiled=True)  58.8 us
    unnamed x5, waiting for transfers between devices  44.3 us
    all_to_all x1, waiting for transfers between devices, swap_down(): return lax.all_to_all(part, 'tp', split_axis=0, concat_axis=1, tiled=True)  37.7 us
    unnamed x48, local copies, waits for them, and re-layouts  27.7 us
    all_to_all x1, blocking collectives, swap_up(): lax.all_to_all(part, axis_name, split_axis=1, concat_axis=0, tiled=True)  22.1 us
    all_to_all x1, waiting for transfers between devices, shards(): lax.all_to_all(placed_rows.reshape(groups, cap, narrow), 'fsdp', split_ax...  19.5 us
  transfers between devices with their start and end apart: 15, of which 14 were waited for; matrix products, arithmetic and copies ran while one was open for 8% of the time, Pallas kernels for 0%

profile of v1, /device:TPU:0, one launch (start us, length us, event | category | flops | bytes accessed | tf_op | source)
XLA Modules:
  0.0 536.2 jit_solution(11191175972309176641)
XLA Ops:
  7.2 2.1 pad.4
  9.2 5.2 all-to-all-start
  15.2 11.8 %all-to-all-done = bf16[8,96,512]{2,1,0:T(8,128)(2,1)S(1)} async-done(((bf16[8,96,512]{2,1,0:T(8,128)(2,1)}), bf16[8,96,512]{2,1,0:T(8,128)(2,1)S(1)}, u32[]{:S(2)}, u32[]{:S(2)}) %all-to-all-start) | async-done | bytes 786464 | tf_op jit(solution)/shard_map/all_to_all | solution.py:71
  28.1 1.9 reshape.196
  30.4 2.0 multiply_convert_fusion
  32.6 22.1 %all_to_all.135 = bf16[96,4,1024]{2,0,1:T(8,128)(2,1)} all-to-all(bf16[96,4,1024]{2,0,1:T(8,128)(2,1)S(1)} %copy.58), channel_id=1, replica_groups=mesh['fsdp'=4,'tp'=8] {'fsdp'}, dimensions={1} | all-to-all | bytes 1572864 | tf_op jit(solution)/shard_map/all_to_all | solution.py:37
  55.4 4.8 all-to-all-start.3
  60.2 2.9 copy.60
  63.0 2.1 all-to-all-done.3
  65.2 4.6 all-to-all-start.2
  69.8 9.2 %all-gather = s32[4,1,9]{2,1,0:T(1,128)S(1)} all-gather(s32[1,1,9]{2,1,0:T(1,128)S(1)} %bitcast.122), channel_id=1, replica_groups=mesh['fsdp'=4,'tp'=8] {'fsdp'}, dimensions={0}, use_global_device_ids=true | all-gather | bytes 180 | tf_op jit(solution)/shard_map/all_gather | solution.py:77
  79.2 2.1 constant_dynamic-slice_fusion.1
  81.3 2.9 copy.73
  85.1 2.6 fusion.34
  87.8 34.8 %all-to-all-done.2 = bf16[128,8,1536]{0,2,1:T(8,128)(2,1)} async-done(((bf16[128,8,1536]{0,2,1:T(8,128)(2,1)}), bf16[128,8,1536]{0,2,1:T(8,128)(2,1)}, u32[]{:S(2)}, u32[]{:S(2)}) %all-to-all-start.2) | async-done | bytes 3145760 | tf_op jit(solution)/shard_map/all_to_all | solution.py:37
  122.6 3.9 fusion.7
  126.6 12.5 %fusion.15 = bf16[1536,1024]{1,0:T(8,128)(2,1)S(1)} fusion(bf16[3072,1024]{1,0:T(8,128)(2,1)} %all-gather.3.cloned.1.call-done, s32[1536]{0:T(1024)S(1)} %fusion.32), kind=kOutput, calls=%fused_computation.22 | convolution fusion | flops 9669967872 | bytes 9443328 | tf_op jit(solution)/shard_map/dot_general | solution.py:89
  139.1 1.6 copy-done.12
  140.7 6.9 %convolution_convert_fusion.1 = bf16[1536,1536]{1,0:T(8,128)(2,1)} fusion(bf16[1536,1024]{1,0:T(8,128)(2,1)S(1)} %fusion.15, bf16[1024,1536]{0,1:T(8,128)(2,1)S(1)} %fusion.7), kind=kOutput, calls=%fused_computation.7 | convolution fusion | flops 4834197504 | bytes 11010048 | tf_op jit(solution)/shard_map/dot_general | solution.py:94
  149.0 3.4 all-to-all-start.5
  152.4 2.8 copy.64
  155.2 2.1 all-to-all-done.5
  157.4 4.5 all-to-all-start.4
  162.1 2.1 constant_dynamic-slice_fusion
  164.2 2.9 copy.74
  167.2 32.5 %all-to-all-done.4 = bf16[128,8,1536]{0,2,1:T(8,128)(2,1)} async-done(((bf16[128,8,1536]{0,2,1:T(8,128)(2,1)}), bf16[128,8,1536]{0,2,1:T(8,128)(2,1)}, u32[]{:S(2)}, u32[]{:S(2)}) %all-to-all-start.4) | async-done | bytes 3145760 | tf_op jit(solution)/shard_map/all_to_all | solution.py:37
  199.7 4.0 fusion.5
  203.7 6.9 %convolution_convert_fusion = bf16[1536,1536]{1,0:T(8,128)(2,1)} fusion(bf16[1536,1024]{1,0:T(8,128)(2,1)S(1)} %copy-done.13, bf16[1024,1536]{0,1:T(8,128)(2,1)S(1)} %fusion.5), kind=kOutput, calls=%fused_computation.6 | convolution fusion | flops 4834197504 | bytes 11010048 | tf_op jit(solution)/shard_map/dot_general | solution.py:95
  211.5 7.4 %all_to_all.136 = f32[8,12,128]{2,1,0:T(8,128)S(1)} all-to-all(f32[8,12,128]{2,1,0:T(8,128)S(1)} %all_to_all.119), channel_id=1, replica_groups=mesh['fsdp'=4,'tp'=8] {'tp'}, dimensions={0} | all-to-all | bytes 98304 | tf_op jit(solution)/shard_map/all_to_all | solution.py:41
  218.8 3.7 all-to-all-start.6
  222.6 37.7 %all-to-all-done.6 = bf16[8,1536,128]{2,1,0:T(8,128)(2,1)S(1)} async-done(((bf16[8,1536,128]{2,1,0:T(8,128)(2,1)}), bf16[8,1536,128]{2,1,0:T(8,128)(2,1)S(1)}, u32[]{:S(2)}, u32[]{:S(2)}) %all-to-all-start.6) | async-done | bytes 3145760 | tf_op jit(solution)/shard_map/all_to_all | solution.py:41
  260.3 2.1 copy_bitcast_fusion
  262.4 58.8 %reduce-scatter.8.cloned.1.call-done = bf16[384,1536]{1,0:T(8,128)(2,1)} async-done(((bf16[1536,1536]{1,0:T(8,128)(2,1)}), bf16[384,1536]{1,0:T(8,128)(2,1)}) %reduce-scatter.8.cloned.1.call-update) | async-done | bytes 1179664 | tf_op jit(solution)/shard_map/reduce_scatter | solution.py:98
  321.2 2.4 fusion.21
  324.6 1.5 collective-permute-start
  326.1 28.0 %collective-permute-done = bf16[384,1536]{1,0:T(8,128)(2,1)S(1)} collective-permute-done((bf16[384,1536]{1,0:T(8,128)(2,1)S(1)}, bf16[384,1536]{1,0:T(8,128)(2,1)S(1)}, u32[]{:S(2)}, u32[]{:S(2)}) %collective-permute-start) | collective-permute-done | bytes 1179680 | tf_op jit(solution)/shard_map/ppermute | solution.py:16
  355.1 28.7 %collective-permute-done.1 = bf16[384,1536]{1,0:T(8,128)(2,1)} collective-permute-done((bf16[384,1536]{1,0:T(8,128)(2,1)S(1)}, bf16[384,1536]{1,0:T(8,128)(2,1)}, u32[]{:S(2)}, u32[]{:S(2)}) %collective-permute-start.1) | collective-permute-done | bytes 1179680 | tf_op jit(solution)/shard_map/ppermute | solution.py:16
  383.8 3.4 fusion.9
  387.3 24.6 %collective-permute-done.2 = bf16[384,1536]{1,0:T(8,128)(2,1)} collective-permute-done((bf16[384,1536]{1,0:T(8,128)(2,1)}, bf16[384,1536]{1,0:T(8,128)(2,1)}, u32[]{:S(2)}, u32[]{:S(2)}) %collective-permute-start.2) | collective-permute-done | bytes 1179680 | tf_op jit(solution)/shard_map/ppermute | solution.py:16
  417.6 5.3 fusion.12
  422.9 3.0 copy.71
  426.0 44.2 %reduce-scatter.10.cloned.1.call-done = bf16[128,1536]{1,0:T(8,128)(2,1)} async-done(((bf16[1024,1536]{1,0:T(8,128)(2,1)}), bf16[128,1536]{1,0:T(8,128)(2,1)}) %reduce-scatter.10.cloned.1.call-update) | async-done | bytes 393232
  470.3 5.5 %fusion.16 = bf16[3008,128]{1,0:T(8,128)(2,1)} fusion(s32[3008]{0:T(1024)S(1)} %select_n.98, bf16[128,1536]{1,0:T(8,128)(2,1)} %reduce-scatter.10.cloned.1.call-done), kind=kOutput, calls=%fused_computation.23 | convolution fusion | flops 1187799040 | bytes 1175296 | tf_op jit(solution)/shard_map/dot_general | solution.py:114
  475.8 4.7 all-to-all-start.8
  480.6 19.5 %all-to-all-done.8 = bf16[4,752,128]{2,1,0:T(8,128)(2,1)S(1)} async-done(((bf16[4,752,128]{2,1,0:T(8,128)(2,1)}), bf16[4,752,128]{2,1,0:T(8,128)(2,1)S(1)}, u32[]{:S(2)}, u32[]{:S(2)}) %all-to-all-start.8) | async-done | bytes 770080 | tf_op jit(solution)/shard_map/all_to_all | solution.py:115
  501.5 3.6 all-to-all-start.9
  507.6 18.0 %all-to-all-done.9 = bf16[8,752,128]{2,1,0:T(8,128)(2,1)S(1)} async-done(((bf16[8,752,128]{2,1,0:T(8,128)(2,1)}), bf16[8,752,128]{2,1,0:T(8,128)(2,1)S(1)}, u32[]{:S(2)}, u32[]{:S(2)}) %all-to-all-start.9) | async-done | bytes 1540128 | tf_op jit(solution)/shard_map/all_to_all | solution.py:123
  526.2 1.4 fusion.24
  (88 shorter events, 21.5 us)
Async XLA Ops:
  9.2 17.8 %all-to-all-start = ((bf16[8,96,512]{2,1,0:T(8,128)(2,1)}), bf16[8,96,512]{2,1,0:T(8,128)(2,1)S(1)}, u32[]{:S(2)}, u32[]{:S(2)}) async-start(bf16[8,96,512]{2,1,0:T(8,128)(2,1)} %bitcast.7), calls=%async_computation | async-start | bytes 1572864 | tf_op jit(solution)/shard_map/all_to_all | solution.py:71
  14.4 112.1 %all-gather.3.cloned.1.call-start = ((), (), s32[]{:S(2)}) async-start(), calls=%async_computation.13 | async-start | bytes 7077888 | tf_op jit(solution)/shard_map/all_gather | solution.py:76
  30.3 24.4 %copy-start.8 = (f32[128,96]{0,1:T(8,128)S(1)}, f32[128,96]{0,1:T(8,128)}, u32[]{:S(2)}) copy-start(f32[128,96]{0,1:T(8,128)} %param.19) | copy-start | bytes 147460
  30.3 29.8 %copy-start.5 = (bf16[128,12288]{1,0:T(8,128)(2,1)S(1)}, bf16[128,12288]{1,0:T(8,128)(2,1)}, u32[]{:S(2)}) copy-start(bf16[128,12288]{1,0:T(8,128)(2,1)} %param.17) | copy-start | bytes 9437188
  55.4 9.8 %all-to-all-start.3 = ((f32[128,8,12]{0,2,1:T(8,128)}), f32[128,8,12]{0,2,1:T(8,128)S(1)}, u32[]{:S(2)}, u32[]{:S(2)}) async-start(f32[128,8,12]{0,2,1:T(8,128)} %all_to_all.107), calls=%async_computation.3 | async-start | bytes 131072 | tf_op jit(solution)/shard_map/all_to_all | solution.py:37
  65.2 4.7 copy-start.11
  65.2 57.4 %all-to-all-start.2 = ((bf16[128,8,1536]{0,2,1:T(8,128)(2,1)}), bf16[128,8,1536]{0,2,1:T(8,128)(2,1)}, u32[]{:S(2)}, u32[]{:S(2)}) async-start(bf16[128,8,1536]{0,2,1:T(8,128)(2,1)} %bitcast.11), calls=%async_computation.2 | async-start | bytes 6291456 | tf_op jit(solution)/shard_map/all_to_all | solution.py:37
  69.8 192.6 %reduce-scatter.6.cloned.1.call-start = ((), (), s32[]{:S(2)}) async-start(), calls=%async_computation.14 | async-start | bytes 5898240 | tf_op jit(solution)/shard_map/reduce_scatter | solution.py:97
  139.1 1.6 copy-start.12
  147.6 0.8 copy-start.9
  147.6 4.8 copy-start.6
  149.0 8.3 %all-to-all-start.5 = ((f32[128,8,12]{0,2,1:T(8,128)}), f32[128,8,12]{0,2,1:T(8,128)S(1)}, u32[]{:S(2)}, u32[]{:S(2)}) async-start(f32[128,8,12]{0,2,1:T(8,128)} %all_to_all.112), calls=%async_computation.6 | async-start | bytes 131072 | tf_op jit(solution)/shard_map/all_to_all | solution.py:37
  157.4 42.4 %all-to-all-start.4 = ((bf16[128,8,1536]{0,2,1:T(8,128)(2,1)}), bf16[128,8,1536]{0,2,1:T(8,128)(2,1)}, u32[]{:S(2)}, u32[]{:S(2)}) async-start(bf16[128,8,1536]{0,2,1:T(8,128)(2,1)} %bitcast.15), calls=%async_computation.5 | async-start | bytes 6291456 | tf_op jit(solution)/shard_map/all_to_all | solution.py:37
  161.9 159.4 %reduce-scatter.8.cloned.1.call-start = ((), (), s32[]{:S(2)}) async-start(), calls=%async_computation.15 | async-start | bytes 5898240 | tf_op jit(solution)/shard_map/reduce_scatter | solution.py:98
  199.7 4.0 copy-start.13
  210.7 0.8 copy-start.10
  218.8 41.4 %all-to-all-start.6 = ((bf16[8,1536,128]{2,1,0:T(8,128)(2,1)}), bf16[8,1536,128]{2,1,0:T(8,128)(2,1)S(1)}, u32[]{:S(2)}, u32[]{:S(2)}) async-start(bf16[8,1536,128]{2,1,0:T(8,128)(2,1)} %bitcast.107), calls=%async_computation.8 | async-start | bytes 6291456 | tf_op jit(solution)/shard_map/all_to_all | solution.py:41
  222.5 247.8 %reduce-scatter.10.cloned.1.call-start = ((), (), s32[]{:S(2)}) async-start(), calls=%async_computation.16 | async-start | bytes 3538944
  262.4 121.4 %copy-start = (bf16[1536,1024]{1,0:T(8,128)(2,1)S(1)}, bf16[1536,1024]{1,0:T(8,128)(2,1)}, u32[]{:S(2)}) copy-start(bf16[1536,1024]{1,0:T(8,128)(2,1)} %copy_bitcast_fusion) | copy-start | bytes 9437188
  323.6 1.0 copy-start.1
  324.6 29.4 %collective-permute-start = (bf16[384,1536]{1,0:T(8,128)(2,1)S(1)}, bf16[384,1536]{1,0:T(8,128)(2,1)S(1)}, u32[]{:S(2)}, u32[]{:S(2)}) collective-permute-start(bf16[384,1536]{1,0:T(8,128)(2,1)S(1)} %fusion.21), channel_id=1, source_target_pairs={{0,8},{8,16},{16,24},{24,0},{1,9},{9,17},{17,25},{25,1},{2,10},{10... | collective-permute-start | bytes 3538952 | tf_op jit(solution)/shard_map/ppermute | solution.py:16
  354.1 1.0 copy-start.3
  355.1 28.7 %collective-permute-start.1 = (bf16[384,1536]{1,0:T(8,128)(2,1)S(1)}, bf16[384,1536]{1,0:T(8,128)(2,1)}, u32[]{:S(2)}, u32[]{:S(2)}) collective-permute-start(bf16[384,1536]{1,0:T(8,128)(2,1)S(1)} %collective-permute-done), channel_id=1, source_target_pairs={{0,8},{8,16},{16,24},{24,0},{1,9},{9,17},{17,25},{25,1},{2,10},{10... | collective-permute-start | bytes 3538952 | tf_op jit(solution)/shard_map/ppermute | solution.py:16
  383.8 28.0 %collective-permute-start.2 = (bf16[384,1536]{1,0:T(8,128)(2,1)}, bf16[384,1536]{1,0:T(8,128)(2,1)}, u32[]{:S(2)}, u32[]{:S(2)}) collective-permute-start(bf16[384,1536]{1,0:T(8,128)(2,1)} %collective-permute-done.1), channel_id=1, source_target_pairs={{0,8},{8,16},{16,24},{24,0},{1,9},{9,17},{17,25},{25,1},{2,10},{10... | collective-permute-start | bytes 3538952 | tf_op jit(solution)/shard_map/ppermute | solution.py:16
  387.2 27.3 %copy-start.4 = (bf16[384,1536]{1,0:T(8,128)(2,1)S(1)}, bf16[384,1536]{1,0:T(8,128)(2,1)}, u32[]{:S(2)}) copy-start(bf16[384,1536]{1,0:T(8,128)(2,1)} %copy-done.3) | copy-start | bytes 3538948
  387.2 27.4 %copy-start.2 = (bf16[384,1536]{1,0:T(8,128)(2,1)S(1)}, bf16[384,1536]{1,0:T(8,128)(2,1)}, u32[]{:S(2)}) copy-start(bf16[384,1536]{1,0:T(8,128)(2,1)} %copy-done.1) | copy-start | bytes 3538948
  475.8 29.3 %copy-start.7 = (bf16[752,512]{1,0:T(8,128)(2,1)S(1)}, bf16[752,512]{1,0:T(8,128)(2,1)}, u32[]{:S(2)}) copy-start(bf16[752,512]{1,0:T(8,128)(2,1)} %param.12) | copy-start | bytes 2310148
  475.8 24.3 %all-to-all-start.8 = ((bf16[4,752,128]{2,1,0:T(8,128)(2,1)}), bf16[4,752,128]{2,1,0:T(8,128)(2,1)S(1)}, u32[]{:S(2)}, u32[]{:S(2)}) async-start(bf16[4,752,128]{2,1,0:T(8,128)(2,1)} %bitcast.23), calls=%async_computation.10 | async-start | bytes 1540096 | tf_op jit(solution)/shard_map/all_to_all | solution.py:115
  501.5 24.2 %all-to-all-start.9 = ((bf16[8,752,128]{2,1,0:T(8,128)(2,1)}), bf16[8,752,128]{2,1,0:T(8,128)(2,1)S(1)}, u32[]{:S(2)}, u32[]{:S(2)}) async-start(bf16[8,752,128]{2,1,0:T(8,128)(2,1)} %bitcast_select_fusion), calls=%async_computation.11 | async-start | bytes 3080192 | tf_op jit(solution)/shard_map/all_to_all | solution.py:123
Sparse Core Ops, SparseCore 0:
  54.9 71.6 all-gather.2
  147.8 85.2 reduce-scatter.5
  235.4 85.7 reduce-scatter.7
  426.0 44.2 reduce-scatter.9
